TPU v7x, 256 devices: a whole 4x4x8 slice. The times are simulated.
256 devices in a mesh: row: 32 (over x, y, core), col: 8 (over z).
Axes of the slice: x: 4, y: 4, z: 8, core: 2. Of those that a mesh axis runs over, the one named last changes fastest.
Arguments:
- matrix: float32 [5120, 5120], P('row', 'col'), may hold values from -64 to 64
Outputs:
- iterate: float32 [5120, 5120], P('row', 'col')
- trace_value: float32 [2], replicated
- frobenius: float32 [2], replicated
All inputs are finite; a program needn't handle non-finite values.
Results may differ from a plain program's by a relative error of at most 0.003.
Values may be sent and summed in bfloat16 or wider, within the bound.
No kernel may reach another device: no remote copies, remote signals or barrier semaphores. Data moves between devices by JAX's collectives and lax.ppermute only.
A program may use at most 64 MiB of HBM per device.

v0:
```python
import jax
import jax.numpy as jnp
from jax import lax
from jax.sharding import Mesh
from jax.sharding import PartitionSpec as P

ITERS = 2
ROW = ("row_0", "row_1", "row_2")
ROW_COL = ("row_0", "row_1", "row_2", "col")
target = 0.0625


def from_everyone(shard, axis):
    peers = lax.axis_size(axis)
    return lax.all_to_all(
        jnp.broadcast_to(shard[None], (peers, *shard.shape)), axis, 0, 0, tiled=True
    )


def in_order(pieces, dim):
    shape = list(pieces.shape[1:])
    shape[dim] *= pieces.shape[0]
    return jnp.moveaxis(pieces, 0, dim).reshape(shape)


def collect(shard, axis, dim):
    pieces = from_everyone(shard, axis)
    return in_order(pieces, dim)


def over_axes(shard, axes):
    for axis in axes:
        shard = lax.psum(shard, axis)
    return shard


def add_rows(portion, right_panel):
    return jnp.dot(portion, right_panel, preferred_element_type=jnp.float32)


def on_device(matrix):
    rounded = matrix.astype(jnp.bfloat16)
    current = rounded.astype(jnp.float32)
    row_ids = lax.axis_index(ROW) * matrix.shape[0] + lax.broadcasted_iota(
        jnp.int32, matrix.shape, 0
    )
    col_ids = lax.axis_index("col") * matrix.shape[1] + lax.broadcasted_iota(
        jnp.int32, matrix.shape, 1
    )
    on_diagonal = row_ids == col_ids
    traces = []
    norms = []
    for step in range(ITERS):
        row_panel = collect(rounded, "col", 1)
        if step == 0:
            order_full = row_panel.shape[1]
            squares = over_axes(jnp.sum(current * current), ROW_COL)
            scale = target * order_full / (squares + 1e-06)
            root = jnp.sqrt(scale)
        else:
            scale = jnp.float32(1.0)
            root = jnp.float32(1.0)
        kept_panel = lax.all_gather(rounded, ROW, axis=0, tiled=True)
        product = jnp.dot(row_panel, kept_panel, preferred_element_type=jnp.float32)
        squared = (product * scale).astype(jnp.bfloat16)
        cubic_part = add_rows(
            lax.all_gather(squared, "col", axis=1, tiled=True), right_panel=kept_panel
        )
        current = root * (1.5 * current - 0.5 * cubic_part)
        rounded = current.astype(jnp.bfloat16)
        diagonal_part = jnp.sum(jnp.where(on_diagonal, current, 0.0))
        square_part = jnp.sum(current * current)
        trace_now, total_now = (over_axes(diagonal_part, ROW_COL), over_axes(square_part, ROW_COL))
        traces.append(trace_now)
        norms.append(jnp.sqrt(total_now))
    return (current, jnp.stack(traces), jnp.stack(norms))


def solution(mesh):
    split = Mesh(
        mesh.devices.reshape(4, 4, 2, mesh.shape["col"]), ("row_0", "row_1", "row_2", "col")
    )
    return jax.shard_map(
        on_device,
        mesh=split,
        in_specs=(P(ROW, "col"),),
        out_specs=(P(ROW, "col"), P(), P()),
        check_vma=False,
    )
```

profile of v0, /device:TPU:32, one launch (start us, length us, event | category | flops | bytes accessed | tf_op | source)
XLA Modules:
  0.0 274.8 jit_solution(13605825605742799116)
XLA Ops:
  7.2 0.0 all-gather.5.cloned.1.call-start
  7.2 2.3 fusion.4
  9.5 0.0 all-gather.5.cloned.1.call-update
  9.5 2.2 broadcast_in_dim.9
  11.8 8.6 %all-to-all-start = ((bf16[8,160,640]{2,1,0:T(8,128)(2,1)}), bf16[8,160,640]{2,1,0:T(8,128)(2,1)S(1)}, u32[]{:S(2)}, u32[]{:S(2)}) async-start(bf16[8,160,640]{2,1,0:T(8,128)(2,1)} %broadcast_in_dim.9), calls=%async_computation | async-start | bytes 3276800 | tf_op jit(solution)/shard_map/all_to_all | solution.py:15
  20.3 0.0 all-gather.7.cloned.1.call-start
  20.4 11.1 %psum.140 = f32[]{:T(128)} all-reduce(f32[]{:T(128)} %get-tuple-element.23), channel_id=1, replica_groups=mesh['row_0'=4,'row_1'=4,'row_2'=2,'col'=8] {'row_0'}, use_global_device_ids=true, to_apply=%region_1.0 | all-reduce | flops 1 | bytes 8 | tf_op jit(solution)/shard_map/psum | solution.py:33
  31.5 11.4 %psum.141 = f32[]{:T(128)} all-reduce(f32[]{:T(128)} %psum.140), channel_id=1, replica_groups=mesh['row_0'=4,'row_1'=4,'row_2'=2,'col'=8] {'row_1'}, use_global_device_ids=true, to_apply=%region_2.0 | all-reduce | flops 1 | bytes 8 | tf_op jit(solution)/shard_map/psum | solution.py:33
  42.8 3.1 %psum.142 = f32[]{:T(128)} all-reduce(f32[]{:T(128)} %psum.141), channel_id=1, replica_groups=mesh['row_0'=4,'row_1'=4,'row_2'=2,'col'=8] {'row_2'}, use_global_device_ids=true, to_apply=%region_3.0 | all-reduce | flops 1 | bytes 8 | tf_op jit(solution)/shard_map/psum | solution.py:33
  45.9 20.6 %psum.143 = f32[]{:T(128)} all-reduce(f32[]{:T(128)} %psum.142), channel_id=1, replica_groups=mesh['row_0'=4,'row_1'=4,'row_2'=2,'col'=8] {'col'}, use_global_device_ids=true, to_apply=%region_4.0 | all-reduce | flops 1 | bytes 8 | tf_op jit(solution)/shard_map/psum | solution.py:33
  67.2 0.0 all-to-all-done
  67.2 0.2 copy.6
  67.5 0.7 all-gather.5.cloned.1.call-done
  68.2 0.0 copy-start
  68.2 5.0 %fusion.3 = bf16[160,640]{1,0:T(8,128)(2,1)} fusion(bf16[160,5120]{1,0:T(8,128)(2,1)S(1)} %bitcast.18, bf16[5120,640]{1,0:T(8,128)(2,1)} %all-gather.5.cloned.1.call-done, f32[]{:T(128)S(6)} %div.3), kind=kOutput, calls=%fused_computation.6 | convolution fusion | flops 1048780800 | bytes 8396804 | tf_op jit(solution)/shard_map/dot_general | solution.py:64
  73.2 0.0 all-gather.7.cloned.1.call-update
  73.2 0.0 all-gather.9.cloned.1.call-start
  73.3 41.0 %all-gather.7.cloned.1.call-done = bf16[160,5120]{1,0:T(8,128)(2,1)} async-done(((bf16[160,640]{1,0:T(8,128)(2,1)}), bf16[160,5120]{1,0:T(8,128)(2,1)}) %all-gather.7.cloned.1.call-update) | async-done | bytes 1638416 | tf_op jit(solution)/shard_map/all_gather | solution.py:67
  114.3 0.0 copy-done
  114.3 6.1 %multiply_reduce_fusion.1 = (f32[]{:T(128)}, f32[]{:T(128)}, bf16[160,640]{1,0:T(8,128)(2,1)}, f32[160,640]{1,0:T(8,128)S(1)}) fusion(s32[640]{0:T(1024)S(1)} %iota_add_fusion, s32[160]{0:T(256)S(1)} %iota_add_fusion.1, bf16[160,5120]{1,0:T(8,128)(2,1)} %all-gather.7.cloned.1.call-done, bf16[5120,640]{1,0:T(8,128)(2,1)} %all-gather.5.cloned.1.call-done, ...), kind=kOutput, calls=%fused_computation.16 | convolution fusion | flops 1049702400 | bytes 9014412 | tf_op jit(solution)/shard_map/dot_general | solution.py:38
  120.5 0.0 all-gather.9.cloned.1.call-update
  120.5 0.0 all-gather.11.cloned.1.call-start
  120.5 1.1 broadcast_in_dim.18
  121.6 40.6 %all_to_all.10 = bf16[8,160,640]{2,1,0:T(8,128)(2,1)S(1)} all-to-all(bf16[8,160,640]{2,1,0:T(8,128)(2,1)S(1)} %broadcast_in_dim.18), channel_id=1, replica_groups=mesh['row_0'=4,'row_1'=4,'row_2'=2,'col'=8] {'col'}, dimensions={0} | all-to-all | bytes 3276800 | tf_op jit(solution)/shard_map/all_to_all | solution.py:15
  162.2 0.2 copy.7
  162.4 11.6 %all-gather.9.cloned.1.call-done = bf16[5120,640]{1,0:T(8,128)(2,1)} async-done(((bf16[160,640]{1,0:T(8,128)(2,1)}), bf16[5120,640]{1,0:T(8,128)(2,1)}) %all-gather.9.cloned.1.call-update) | async-done | bytes 6553616 | tf_op jit(solution)/shard_map/all_gather | solution.py:63
  174.0 5.0 %convolution_convert_fusion = bf16[160,640]{1,0:T(8,128)(2,1)} fusion(bf16[160,5120]{1,0:T(8,128)(2,1)S(1)} %bitcast.19, bf16[5120,640]{1,0:T(8,128)(2,1)} %all-gather.9.cloned.1.call-done), kind=kOutput, calls=%fused_computation.7 | convolution fusion | flops 1048678400 | bytes 8396800 | tf_op jit(solution)/shard_map/dot_general | solution.py:64
  179.0 0.0 all-gather.11.cloned.1.call-update
  179.0 38.3 %all-gather.11.cloned.1.call-done = bf16[160,5120]{1,0:T(8,128)(2,1)} async-done(((bf16[160,640]{1,0:T(8,128)(2,1)}), bf16[160,5120]{1,0:T(8,128)(2,1)}) %all-gather.11.cloned.1.call-update) | async-done | bytes 1638416 | tf_op jit(solution)/shard_map/all_gather | solution.py:67
  217.3 6.2 %multiply_reduce_fusion = (f32[]{:T(128)}, f32[]{:T(128)}, f32[160,640]{1,0:T(8,128)}) fusion(s32[640]{0:T(1024)S(1)} %iota_add_fusion, s32[160]{0:T(256)S(1)} %iota_add_fusion.1, bf16[160,5120]{1,0:T(8,128)(2,1)} %all-gather.11.cloned.1.call-done, bf16[5120,640]{1,0:T(8,128)(2,1)} %all-gather.9.cloned.1.call-done, f32[160,640]{1,0:T(8,128)S(1)} %get-tuple-element.26), kind=kOutput, calls=%fused_computation.15 | convolution fusion | flops 1049395200 | bytes 9014408 | tf_op jit(solution)/shard_map/dot_general | solution.py:38
  223.5 11.1 %all-reduce.2 = (f32[]{:T(128)}, f32[]{:T(128)}, f32[]{:T(128)}, f32[]{:T(128)}) all-reduce(f32[]{:T(128)} %get-tuple-element.6, f32[]{:T(128)} %get-tuple-element.4, f32[]{:T(128)} %get-tuple-element.5, f32[]{:T(128)} %get-tuple-element.3), channel_id=1, replica_groups=mesh['row_0'=4,'row_1'=4,'row_2'=2,'col'=8] {'row_0'}, use_global_device_ids=true, to_apply=%region_11.12 | all-reduce | flops 4 | bytes 32 | tf_op jit(solution)/shard_map/psum | solution.py:33
  234.6 11.1 %all-reduce.1 = (f32[]{:T(128)}, f32[]{:T(128)}, f32[]{:T(128)}, f32[]{:T(128)}) all-reduce(f32[]{:T(128)} %get-tuple-element.15, f32[]{:T(128)} %get-tuple-element.16, f32[]{:T(128)} %get-tuple-element.17, f32[]{:T(128)} %get-tuple-element.18), channel_id=1, replica_groups=mesh['row_0'=4,'row_1'=4,'row_2'=2,'col'=8] {'row_1'}, use_global_device_ids=true, to_apply=%region_12.13 | all-reduce | flops 4 | bytes 32 | tf_op jit(solution)/shard_map/psum | solution.py:33
  245.7 3.2 %all-reduce.3 = (f32[]{:T(128)}, f32[]{:T(128)}, f32[]{:T(128)}, f32[]{:T(128)}) all-reduce(f32[]{:T(128)} %get-tuple-element.11, f32[]{:T(128)} %get-tuple-element.12, f32[]{:T(128)} %get-tuple-element.13, f32[]{:T(128)} %get-tuple-element.14), channel_id=1, replica_groups=mesh['row_0'=4,'row_1'=4,'row_2'=2,'col'=8] {'row_2'}, use_global_device_ids=true, to_apply=%region_13.14 | all-reduce | flops 4 | bytes 32 | tf_op jit(solution)/shard_map/psum | solution.py:33
  248.9 16.1 %all-reduce = (f32[1]{0:T(128)}, f32[1]{0:T(128)}, f32[]{:T(128)}, f32[]{:T(128)}) all-reduce(f32[1]{0:T(128)} %bitcast.3, f32[1]{0:T(128)} %bitcast.2, f32[]{:T(128)} %get-tuple-element.21, f32[]{:T(128)} %get-tuple-element.22), channel_id=1, replica_groups=mesh['row_0'=4,'row_1'=4,'row_2'=2,'col'=8] {'col'}, use_global_device_ids=true, to_apply=%region_14.15 | all-reduce | flops 4 | bytes 32 | tf_op jit(solution)/shard_map/psum | solution.py:33
  266.4 1.9 pad_maximum_fusion
  (2 shorter events, 0.0 us)
Async XLA Ops:
  7.2 61.0 %all-gather.5.cloned.1.call-start = ((), (), s32[]{:S(2)}) async-start(), calls=%async_computation.2 | async-start | bytes 6758400 | tf_op jit(solution)/shard_map/all_gather | solution.py:63
  11.8 55.4 %all-to-all-start = ((bf16[8,160,640]{2,1,0:T(8,128)(2,1)}), bf16[8,160,640]{2,1,0:T(8,128)(2,1)S(1)}, u32[]{:S(2)}, u32[]{:S(2)}) async-start(bf16[8,160,640]{2,1,0:T(8,128)(2,1)} %broadcast_in_dim.9), calls=%async_computation | async-start | bytes 3276800 | tf_op jit(solution)/shard_map/all_to_all | solution.py:15
  20.3 94.0 %all-gather.7.cloned.1.call-start = ((), (), s32[]{:S(2)}) async-start(), calls=%async_computation.3 | async-start | bytes 1843200 | tf_op jit(solution)/shard_map/all_gather | solution.py:67
  68.2 46.2 %copy-start = (bf16[160,640]{1,0:T(8,128)(2,1)S(1)}, bf16[160,640]{1,0:T(8,128)(2,1)}, u32[]{:S(2)}) copy-start(bf16[160,640]{1,0:T(8,128)(2,1)} %get-tuple-element.24) | copy-start | bytes 614404
  73.2 100.8 %all-gather.9.cloned.1.call-start = ((), (), s32[]{:S(2)}) async-start(), calls=%async_computation.4 | async-start | bytes 6758400 | tf_op jit(solution)/shard_map/all_gather | solution.py:63
  120.5 96.8 %all-gather.11.cloned.1.call-start = ((), (), s32[]{:S(2)}) async-start(), calls=%async_computation.5 | async-start | bytes 1843200 | tf_op jit(solution)/shard_map/all_gather | solution.py:67
Sparse Core Ops, SparseCore 0:
  11.1 57.0 all-gather.4
  73.3 40.9 all-gather.6
  120.6 53.3 all-gather.8
  179.2 38.0 all-gather.10
where the time goes:
time: 275 us
  blocking collectives  128 us (47%)
  waiting for transfers between devices  91.6 us (33%)
  matrix products  22.3 us (8%)
  between operations  15.9 us (6%)
  starting transfers between devices  8.69 us (3%)
  other arithmetic  4.18 us (2%)
  local copies, waits for them, and re-layouts  3.75 us (1%)
    psum x8, blocking collectives, over_axes(): shard = lax.psum(shard, axis)  87.7 us
    all_gather x2, waiting for transfers between devices, on_device(): lax.all_gather(squared, 'col', axis=1, tiled=True)  79.2 us
    all_to_all x1, blocking collectives, from_everyone(): lax.all_to_all(jnp.broadcast_to(shard[None], (peers, *shard.shape)), axis...  40.6 us
    dot_general x2, matrix products, add_rows(): return jnp.dot(portion, right_panel, preferred_element_type=jnp.float32)  12.3 us
    all_gather x2, waiting for transfers between devices, on_device(): kept_panel = lax.all_gather(rounded, ROW, axis=0, tiled=True)  12.3 us
    dot_general x2, matrix products, on_device(): product = jnp.dot(row_panel, kept_panel, preferred_element_type=jnp.float32)  10 us
    all_to_all x1, starting transfers between devices, from_everyone(): lax.all_to_all(jnp.broadcast_to(shard[None], (peers, *shard.shape)), axis...  8.57 us
  transfers between devices with their start and end apart: 5, of which 4 were waited for; matrix products, arithmetic and copies ran while one was open for 1% of the time, Pallas kernels for 0%

commit v1 on v0

--- a/solution.py
+++ b/solution.py
@@ -8,6 +8,27 @@
 ROW = ("row_0", "row_1", "row_2")
 ROW_COL = ("row_0", "row_1", "row_2", "col")
 target = 0.0625
+
+
+def collect_2(shard, axis, dim):
+    size, index, width = (lax.axis_size(axis), lax.axis_index(axis), shard.shape[dim])
+    right = [(i, (i + 1) % size) for i in range(size)]
+    left = [(i, (i - 1) % size) for i in range(size)]
+    out = jnp.zeros((*shard.shape[:dim], size * width, *shard.shape[dim + 1 :]), shard.dtype)
+    out = lax.dynamic_update_slice_in_dim(out, shard, index * width, axis=dim)
+    from_left = from_right = shard
+    middle = size // 2
+    for step in range(1, middle + 1):
+        from_left = lax.ppermute(from_left, axis, right)
+        out = lax.dynamic_update_slice_in_dim(
+            out, from_left, (index - step) % size * width, axis=dim
+        )
+        if step < size - middle:
+            from_right = lax.ppermute(from_right, axis, left)
+            out = lax.dynamic_update_slice_in_dim(
+                out, from_right, (index + step) % size * width, axis=dim
+            )
+    return out
 
 
 def from_everyone(shard, axis):
@@ -63,9 +84,7 @@
         kept_panel = lax.all_gather(rounded, ROW, axis=0, tiled=True)
         product = jnp.dot(row_panel, kept_panel, preferred_element_type=jnp.float32)
         squared = (product * scale).astype(jnp.bfloat16)
-        cubic_part = add_rows(
-            lax.all_gather(squared, "col", axis=1, tiled=True), right_panel=kept_panel
-        )
+        cubic_part = add_rows(collect_2(squared, "col", 1), right_panel=kept_panel)
         current = root * (1.5 * current - 0.5 * cubic_part)
         rounded = current.astype(jnp.bfloat16)
         diagonal_part = jnp.sum(jnp.where(on_diagonal, current, 0.0))

time: 275 us -> 251 us (0.913)
  waiting for transfers between devices: 91.6 us -> 54.2 us
  starting transfers between devices: 8.69 us -> 23.3 us
  matrix products: 22.3 us -> 14.6 us
  blocking collectives: 128 us -> 134 us
    all_gather x2 -> x0, waiting for transfers between devices: 79.2 us -> none  [on_device(): lax.all_gather(squared, 'col', axis=1, tiled=True)]
    ppermute x0 -> x14, waiting for transfers between devices: none -> 40.2 us  [the longest x8 37.4 us: collect_2(): from_left = lax.ppermute(from_left, axis, right)]
    ppermute x0 -> x14, starting transfers between devices: none -> 14.7 us  [the longest x8 10.6 us: collect_2(): from_left = lax.ppermute(from_left, axis, right)]
    dot_general x2, matrix products: 12.3 us -> 5.65 us  [add_rows(): return jnp.dot(portion, right_panel, preferred_element_type=jnp.float32)]
    all_to_all x1, blocking collectives: 40.6 us -> 45.8 us  [from_everyone(): lax.all_to_all(jnp.broadcast_to(shard[None], (peers, *shard.shape)), axis...]
  transfers between devices with their start and end apart: 5 -> 17, of which waited for: 4 -> 14; matrix products, arithmetic and copies ran while one was open for 1% -> 2% of each run, Pallas kernels for 0% -> 0%
where the time goes in v1:
time: 251 us
  blocking collectives  134 us (53%)
  waiting for transfers between devices  54.2 us (22%)
  starting transfers between devices  23.3 us (9%)
  between operations  16.5 us (7%)
  matrix products  14.6 us (6%)
  local copies, waits for them, and re-layouts  4.53 us (2%)
  other arithmetic  4.09 us (2%)
    psum x8, blocking collectives, over_axes(): shard = lax.psum(shard, axis)  87.7 us
    all_to_all x1, blocking collectives, from_everyone(): lax.all_to_all(jnp.broadcast_to(shard[None], (peers, *shard.shape)), axis...  45.8 us
    ppermute x8, waiting for transfers between devices, collect_2(): from_left = lax.ppermute(from_left, axis, right)  37.4 us
    all_gather x2, waiting for transfers between devices, on_device(): kept_panel = lax.all_gather(rounded, ROW, axis=0, tiled=True)  14 us
    ppermute x8, starting transfers between devices, collect_2(): from_left = lax.ppermute(from_left, axis, right)  10.6 us
    dot_general x2, matrix products, on_device(): product = jnp.dot(row_panel, kept_panel, preferred_element_type=jnp.float32)  8.96 us
    all_to_all x1, starting transfers between devices, from_everyone(): lax.all_to_all(jnp.broadcast_to(shard[None], (peers, *shard.shape)), axis...  8.57 us
    dot_general x2, matrix products, add_rows(): return jnp.dot(portion, right_panel, preferred_element_type=jnp.float32)  5.65 us
  transfers between devices with their start and end apart: 17, of which 14 were waited for; matrix products, arithmetic and copies ran while one was open for 2% of the time, Pallas kernels for 0%

profile of v1, /device:TPU:32, one launch (start us, length us, event | category | flops | bytes accessed | tf_op | source)
XLA Modules:
  0.0 250.7 jit_solution(10463118430767447587)
XLA Ops:
  7.2 0.0 all-gather.3.cloned.1.call-start
  7.2 2.3 fusion.3
  9.5 0.0 all-gather.3.cloned.1.call-update
  9.5 2.2 broadcast_in_dim.9
  11.8 8.6 %all-to-all-start = ((bf16[8,160,640]{2,1,0:T(8,128)(2,1)}), bf16[8,160,640]{2,1,0:T(8,128)(2,1)S(1)}, u32[]{:S(2)}, u32[]{:S(2)}) async-start(bf16[8,160,640]{2,1,0:T(8,128)(2,1)} %broadcast_in_dim.9), calls=%async_computation | async-start | bytes 3276800 | tf_op jit(solution)/shard_map/all_to_all | solution.py:36
  20.4 0.0 all-gather.5.cloned.1.call-start
  20.4 11.1 %psum.140 = f32[]{:T(128)} all-reduce(f32[]{:T(128)} %get-tuple-element.23), channel_id=1, replica_groups=mesh['row_0'=4,'row_1'=4,'row_2'=2,'col'=8] {'row_0'}, use_global_device_ids=true, to_apply=%region_1.0 | all-reduce | flops 1 | bytes 8 | tf_op jit(solution)/shard_map/psum | solution.py:54
  31.5 11.4 %psum.141 = f32[]{:T(128)} all-reduce(f32[]{:T(128)} %psum.140), channel_id=1, replica_groups=mesh['row_0'=4,'row_1'=4,'row_2'=2,'col'=8] {'row_1'}, use_global_device_ids=true, to_apply=%region_2.0 | all-reduce | flops 1 | bytes 8 | tf_op jit(solution)/shard_map/psum | solution.py:54
  42.8 3.1 %psum.142 = f32[]{:T(128)} all-reduce(f32[]{:T(128)} %psum.141), channel_id=1, replica_groups=mesh['row_0'=4,'row_1'=4,'row_2'=2,'col'=8] {'row_2'}, use_global_device_ids=true, to_apply=%region_3.0 | all-reduce | flops 1 | bytes 8 | tf_op jit(solution)/shard_map/psum | solution.py:54
  45.9 20.6 %psum.143 = f32[]{:T(128)} all-reduce(f32[]{:T(128)} %psum.142), channel_id=1, replica_groups=mesh['row_0'=4,'row_1'=4,'row_2'=2,'col'=8] {'col'}, use_global_device_ids=true, to_apply=%region_4.0 | all-reduce | flops 1 | bytes 8 | tf_op jit(solution)/shard_map/psum | solution.py:54
  67.3 0.0 all-to-all-done
  67.3 0.2 copy.6
  67.5 0.6 all-gather.3.cloned.1.call-done
  68.1 0.2 broadcast.23.clone
  68.3 0.0 slice-start.3
  68.3 4.5 %constant_dynamic-update-slice_fusion.15 = (bf16[160,5120]{1,0:T(8,128)(2,1)S(1)}, bf16[160,640]{1,0:T(8,128)(2,1)S(1)}) fusion(bf16[160,5120]{1,0:T(8,128)(2,1)S(1)} %broadcast.23.clone, s32[]{:T(128)S(6)} %select_n.84, f32[]{:T(128)S(6)} %div.3, bf16[160,5120]{1,0:T(8,128)(2,1)S(1)} %bitcast.22, bf16[5120,640]{1,0:T(8,128)(2,1)} %all-gather.3.cloned.1.call-done), kind=kOutput, calls=%fused_computation.33 | convolution fusion | flops 1048780800 | bytes 8601608 | tf_op jit(solution)/shard_map/dot_general | solution.py:85
  72.8 0.0 copy-start
  72.8 1.8 collective-permute-start
  74.6 0.3 collective-permute-start.1
  75.0 5.2 %collective-permute-done = bf16[160,640]{1,0:T(8,128)(2,1)S(1)} collective-permute-done((bf16[160,640]{1,0:T(8,128)(2,1)S(1)}, bf16[160,640]{1,0:T(8,128)(2,1)S(1)}, u32[]{:S(2)}, u32[]{:S(2)}) %collective-permute-start) | collective-permute-done | bytes 204832 | tf_op jit(solution)/shard_map/ppermute | solution.py:22
  80.1 1.6 collective-permute-start.2
  81.7 0.0 collective-permute-done.1
  81.7 0.5 collective-permute-start.3
  82.2 4.2 %collective-permute-done.2 = bf16[160,640]{1,0:T(8,128)(2,1)S(1)} collective-permute-done((bf16[160,640]{1,0:T(8,128)(2,1)S(1)}, bf16[160,640]{1,0:T(8,128)(2,1)S(1)}, u32[]{:S(2)}, u32[]{:S(2)}) %collective-permute-start.2) | collective-permute-done | bytes 204832 | tf_op jit(solution)/shard_map/ppermute | solution.py:22
  86.5 1.4 collective-permute-start.4
  87.9 0.4 collective-permute-done.3
  88.3 0.8 collective-permute-start.5
  89.2 3.6 %collective-permute-done.4 = bf16[160,640]{1,0:T(8,128)(2,1)S(1)} collective-permute-done((bf16[160,640]{1,0:T(8,128)(2,1)S(1)}, bf16[160,640]{1,0:T(8,128)(2,1)S(1)}, u32[]{:S(2)}, u32[]{:S(2)}) %collective-permute-start.4) | collective-permute-done | bytes 204832 | tf_op jit(solution)/shard_map/ppermute | solution.py:22
  92.9 1.2 collective-permute-start.6
  94.1 0.9 collective-permute-done.5
  95.0 5.0 %collective-permute-done.6 = bf16[160,640]{1,0:T(8,128)(2,1)S(1)} collective-permute-done((bf16[160,640]{1,0:T(8,128)(2,1)S(1)}, bf16[160,640]{1,0:T(8,128)(2,1)S(1)}, u32[]{:S(2)}, u32[]{:S(2)}) %collective-permute-start.6) | collective-permute-done | bytes 204832 | tf_op jit(solution)/shard_map/ppermute | solution.py:22
  100.1 0.0 slice-done.2
  100.1 0.0 slice-done.3
  100.1 0.0 copy-done
  100.1 2.8 %multiply_reduce_fusion.1 = (f32[]{:T(128)}, f32[]{:T(128)}, bf16[160,640]{1,0:T(8,128)(2,1)}, f32[160,640]{1,0:T(8,128)S(1)}) fusion(s32[640]{0:T(1024)S(1)} %iota_add_fusion, s32[160]{0:T(256)S(1)} %iota_add_fusion.1, bf16[160,5120]{1,0:T(8,128)(2,1)S(1)} %constant_dynamic-update-slice_fusion.8, bf16[5120,640]{1,0:T(8,128)(2,1)S(1)} %bitcast.21, ...), kind=kOutput, calls=%fused_computation.15 | convolution fusion | flops 1049702400 | bytes 9014412 | tf_op jit(solution)/shard_map/dot_general | solution.py:59
  103.0 0.0 all-gather.5.cloned.1.call-update
  103.0 1.1 broadcast_in_dim.18
  104.1 45.8 %all_to_all.10 = bf16[8,160,640]{2,1,0:T(8,128)(2,1)S(1)} all-to-all(bf16[8,160,640]{2,1,0:T(8,128)(2,1)S(1)} %broadcast_in_dim.18), channel_id=1, replica_groups=mesh['row_0'=4,'row_1'=4,'row_2'=2,'col'=8] {'col'}, dimensions={0} | all-to-all | bytes 3276800 | tf_op jit(solution)/shard_map/all_to_all | solution.py:36
  149.8 0.2 copy.7
  150.1 13.4 %all-gather.5.cloned.1.call-done = bf16[5120,640]{1,0:T(8,128)(2,1)} async-done(((bf16[160,640]{1,0:T(8,128)(2,1)}), bf16[5120,640]{1,0:T(8,128)(2,1)}) %all-gather.5.cloned.1.call-update) | async-done | bytes 6553616 | tf_op jit(solution)/shard_map/all_gather | solution.py:84
  163.5 0.2 broadcast.23
  163.6 0.0 slice-start.1
  163.6 4.5 %constant_dynamic-update-slice_fusion.7 = (bf16[160,5120]{1,0:T(8,128)(2,1)S(1)}, bf16[160,640]{1,0:T(8,128)(2,1)S(1)}) fusion(bf16[160,5120]{1,0:T(8,128)(2,1)S(1)} %broadcast.23, s32[]{:T(128)S(6)} %select_n.84, bf16[160,5120]{1,0:T(8,128)(2,1)S(1)} %bitcast.23, bf16[5120,640]{1,0:T(8,128)(2,1)} %all-gather.5.cloned.1.call-done), kind=kOutput, calls=%fused_computation.25 | convolution fusion | flops 1048678400 | bytes 8601604 | tf_op jit(solution)/shard_map/dot_general | solution.py:85
  168.1 1.8 collective-permute-start.7
  169.9 0.5 collective-permute-start.8
  170.4 5.2 %collective-permute-done.7 = bf16[160,640]{1,0:T(8,128)(2,1)S(1)} collective-permute-done((bf16[160,640]{1,0:T(8,128)(2,1)S(1)}, bf16[160,640]{1,0:T(8,128)(2,1)S(1)}, u32[]{:S(2)}, u32[]{:S(2)}) %collective-permute-start.7) | collective-permute-done | bytes 204832 | tf_op jit(solution)/shard_map/ppermute | solution.py:22
  175.6 1.6 collective-permute-start.9
  177.2 0.0 collective-permute-done.8
  177.2 0.5 collective-permute-start.10
  177.7 4.8 %collective-permute-done.9 = bf16[160,640]{1,0:T(8,128)(2,1)S(1)} collective-permute-done((bf16[160,640]{1,0:T(8,128)(2,1)S(1)}, bf16[160,640]{1,0:T(8,128)(2,1)S(1)}, u32[]{:S(2)}, u32[]{:S(2)}) %collective-permute-start.9) | collective-permute-done | bytes 204832 | tf_op jit(solution)/shard_map/ppermute | solution.py:22
  182.5 1.0 collective-permute-start.11
  183.5 0.6 collective-permute-done.10
  184.1 1.4 collective-permute-start.12
  185.6 3.9 %collective-permute-done.11 = bf16[160,640]{1,0:T(8,128)(2,1)S(1)} collective-permute-done((bf16[160,640]{1,0:T(8,128)(2,1)S(1)}, bf16[160,640]{1,0:T(8,128)(2,1)S(1)}, u32[]{:S(2)}, u32[]{:S(2)}) %collective-permute-start.11) | collective-permute-done | bytes 204832 | tf_op jit(solution)/shard_map/ppermute | solution.py:22
  189.5 0.3 collective-permute-start.13
  189.9 0.9 collective-permute-done.12
  190.8 5.4 %collective-permute-done.13 = bf16[160,640]{1,0:T(8,128)(2,1)S(1)} collective-permute-done((bf16[160,640]{1,0:T(8,128)(2,1)S(1)}, bf16[160,640]{1,0:T(8,128)(2,1)S(1)}, u32[]{:S(2)}, u32[]{:S(2)}) %collective-permute-start.13) | collective-permute-done | bytes 204832 | tf_op jit(solution)/shard_map/ppermute | solution.py:22
  196.3 0.0 slice-done
  196.3 2.8 %multiply_reduce_fusion = (f32[]{:T(128)}, f32[]{:T(128)}, f32[160,640]{1,0:T(8,128)}) fusion(s32[640]{0:T(1024)S(1)} %iota_add_fusion, s32[160]{0:T(256)S(1)} %iota_add_fusion.1, bf16[160,5120]{1,0:T(8,128)(2,1)S(1)} %constant_dynamic-update-slice_fusion, bf16[5120,640]{1,0:T(8,128)(2,1)S(1)} %bitcast.19, f32[160,640]{1,0:T(8,128)S(1)} %get-tuple-element.28), kind=kOutput, calls=%fused_computation.14 | convolution fusion | flops 1049395200 | bytes 9014408 | tf_op jit(solution)/shard_map/dot_general | solution.py:59
  199.1 10.2 %all-reduce.2 = (f32[]{:T(128)}, f32[]{:T(128)}, f32[]{:T(128)}, f32[]{:T(128)}) all-reduce(f32[]{:T(128)} %get-tuple-element.6, f32[]{:T(128)} %get-tuple-element.4, f32[]{:T(128)} %get-tuple-element.5, f32[]{:T(128)} %get-tuple-element.3), channel_id=1, replica_groups=mesh['row_0'=4,'row_1'=4,'row_2'=2,'col'=8] {'row_0'}, use_global_device_ids=true, to_apply=%region_11.12 | all-reduce | flops 4 | bytes 32 | tf_op jit(solution)/shard_map/psum | solution.py:54
  209.3 9.9 %all-reduce.1 = (f32[]{:T(128)}, f32[]{:T(128)}, f32[]{:T(128)}, f32[]{:T(128)}) all-reduce(f32[]{:T(128)} %get-tuple-element.15, f32[]{:T(128)} %get-tuple-element.16, f32[]{:T(128)} %get-tuple-element.17, f32[]{:T(128)} %get-tuple-element.18), channel_id=1, replica_groups=mesh['row_0'=4,'row_1'=4,'row_2'=2,'col'=8] {'row_1'}, use_global_device_ids=true, to_apply=%region_12.13 | all-reduce | flops 4 | bytes 32 | tf_op jit(solution)/shard_map/psum | solution.py:54
  219.2 3.1 %all-reduce.3 = (f32[]{:T(128)}, f32[]{:T(128)}, f32[]{:T(128)}, f32[]{:T(128)}) all-reduce(f32[]{:T(128)} %get-tuple-element.11, f32[]{:T(128)} %get-tuple-element.12, f32[]{:T(128)} %get-tuple-element.13, f32[]{:T(128)} %get-tuple-element.14), channel_id=1, replica_groups=mesh['row_0'=4,'row_1'=4,'row_2'=2,'col'=8] {'row_2'}, use_global_device_ids=true, to_apply=%region_13.14 | all-reduce | flops 4 | bytes 32 | tf_op jit(solution)/shard_map/psum | solution.py:54
  222.3 18.4 %all-reduce = (f32[1]{0:T(128)}, f32[1]{0:T(128)}, f32[]{:T(128)}, f32[]{:T(128)}) all-reduce(f32[1]{0:T(128)} %bitcast.3, f32[1]{0:T(128)} %bitcast.2, f32[]{:T(128)} %get-tuple-element.21, f32[]{:T(128)} %get-tuple-element.22), channel_id=1, replica_groups=mesh['row_0'=4,'row_1'=4,'row_2'=2,'col'=8] {'col'}, use_global_device_ids=true, to_apply=%region_14.15 | all-reduce | flops 4 | bytes 32 | tf_op jit(solution)/shard_map/psum | solution.py:54
  242.1 1.8 pad_maximum_fusion
  (21 shorter events, 0.4 us)
Async XLA Ops:
  7.2 61.0 %all-gather.3.cloned.1.call-start = ((), (), s32[]{:S(2)}) async-start(), calls=%async_computation.2 | async-start | bytes 6758400 | tf_op jit(solution)/shard_map/all_gather | solution.py:84
  11.8 55.5 %all-to-all-start = ((bf16[8,160,640]{2,1,0:T(8,128)(2,1)}), bf16[8,160,640]{2,1,0:T(8,128)(2,1)S(1)}, u32[]{:S(2)}, u32[]{:S(2)}) async-start(bf16[8,160,640]{2,1,0:T(8,128)(2,1)} %broadcast_in_dim.9), calls=%async_computation | async-start | bytes 3276800 | tf_op jit(solution)/shard_map/all_to_all | solution.py:36
  20.4 143.1 %all-gather.5.cloned.1.call-start = ((), (), s32[]{:S(2)}) async-start(), calls=%async_computation.3 | async-start | bytes 6758400 | tf_op jit(solution)/shard_map/all_gather | solution.py:84
  68.1 32.0 %slice-start.2 = ((s8[6553600]{0:T(1024)(128)(4,1)}), s8[4194304]{0:T(1024)(128)(4,1)S(1)}, s32[]{:S(2)}) async-start(s8[6553600]{0:T(1024)(128)(4,1)} %bitcast.20), calls=%async_computation.6 | async-start | bytes 8388608
  68.3 31.8 %slice-start.3 = ((s8[6553600]{0:T(1024)(128)(4,1)}), s8[2359296]{0:T(1024)(128)(4,1)S(1)}, s32[]{:S(2)}) async-start(s8[6553600]{0:T(1024)(128)(4,1)} %bitcast.20), calls=%async_computation.7 | async-start | bytes 4718592
  72.8 27.3 %copy-start = (bf16[160,640]{1,0:T(8,128)(2,1)S(1)}, bf16[160,640]{1,0:T(8,128)(2,1)}, u32[]{:S(2)}) copy-start(bf16[160,640]{1,0:T(8,128)(2,1)} %get-tuple-element.24) | copy-start | bytes 614404
  72.8 7.3 %collective-permute-start = (bf16[160,640]{1,0:T(8,128)(2,1)S(1)}, bf16[160,640]{1,0:T(8,128)(2,1)S(1)}, u32[]{:S(2)}, u32[]{:S(2)}) collective-permute-start(bf16[160,640]{1,0:T(8,128)(2,1)S(1)} %get-tuple-element.27), channel_id=1, source_target_pairs={{0,1},{1,2},{2,3},{3,4},{4,5},{5,6},{6,7},{7,0},{8,9},{9,10},{10,1... | collective-permute-start | bytes 614408 | tf_op jit(solution)/shard_map/ppermute | solution.py:22
  74.6 7.1 %collective-permute-start.1 = (bf16[160,640]{1,0:T(8,128)(2,1)S(1)}, bf16[160,640]{1,0:T(8,128)(2,1)S(1)}, u32[]{:S(2)}, u32[]{:S(2)}) collective-permute-start(bf16[160,640]{1,0:T(8,128)(2,1)S(1)} %get-tuple-element.27), channel_id=1, source_target_pairs={{0,7},{1,0},{2,1},{3,2},{4,3},{5,4},{6,5},{7,6},{8,15},{9,8},{10,9... | collective-permute-start | bytes 614408 | tf_op jit(solution)/shard_map/ppermute | solution.py:27
  80.1 6.4 %collective-permute-start.2 = (bf16[160,640]{1,0:T(8,128)(2,1)S(1)}, bf16[160,640]{1,0:T(8,128)(2,1)S(1)}, u32[]{:S(2)}, u32[]{:S(2)}) collective-permute-start(bf16[160,640]{1,0:T(8,128)(2,1)S(1)} %collective-permute-done), channel_id=1, source_target_pairs={{0,1},{1,2},{2,3},{3,4},{4,5},{5,6},{6,7},{7,0},{8,9},{9,10},{10,1... | collective-permute-start | bytes 614408 | tf_op jit(solution)/shard_map/ppermute | solution.py:22
  81.7 6.6 %collective-permute-start.3 = (bf16[160,640]{1,0:T(8,128)(2,1)S(1)}, bf16[160,640]{1,0:T(8,128)(2,1)S(1)}, u32[]{:S(2)}, u32[]{:S(2)}) collective-permute-start(bf16[160,640]{1,0:T(8,128)(2,1)S(1)} %collective-permute-done.1), channel_id=1, source_target_pairs={{0,7},{1,0},{2,1},{3,2},{4,3},{5,4},{6,5},{7,6},{8,15},{9,8},{10,9... | collective-permute-start | bytes 614408 | tf_op jit(solution)/shard_map/ppermute | solution.py:27
  86.5 6.4 %collective-permute-start.4 = (bf16[160,640]{1,0:T(8,128)(2,1)S(1)}, bf16[160,640]{1,0:T(8,128)(2,1)S(1)}, u32[]{:S(2)}, u32[]{:S(2)}) collective-permute-start(bf16[160,640]{1,0:T(8,128)(2,1)S(1)} %collective-permute-done.2), channel_id=1, source_target_pairs={{0,1},{1,2},{2,3},{3,4},{4,5},{5,6},{6,7},{7,0},{8,9},{9,10},{10,1... | collective-permute-start | bytes 614408 | tf_op jit(solution)/shard_map/ppermute | solution.py:22
  88.3 6.7 %collective-permute-start.5 = (bf16[160,640]{1,0:T(8,128)(2,1)S(1)}, bf16[160,640]{1,0:T(8,128)(2,1)S(1)}, u32[]{:S(2)}, u32[]{:S(2)}) collective-permute-start(bf16[160,640]{1,0:T(8,128)(2,1)S(1)} %collective-permute-done.3), channel_id=1, source_target_pairs={{0,7},{1,0},{2,1},{3,2},{4,3},{5,4},{6,5},{7,6},{8,15},{9,8},{10,9... | collective-permute-start | bytes 614408 | tf_op jit(solution)/shard_map/ppermute | solution.py:27
  92.9 7.2 %collective-permute-start.6 = (bf16[160,640]{1,0:T(8,128)(2,1)S(1)}, bf16[160,640]{1,0:T(8,128)(2,1)S(1)}, u32[]{:S(2)}, u32[]{:S(2)}) collective-permute-start(bf16[160,640]{1,0:T(8,128)(2,1)S(1)} %collective-permute-done.4), channel_id=1, source_target_pairs={{0,1},{1,2},{2,3},{3,4},{4,5},{5,6},{6,7},{7,0},{8,9},{9,10},{10,1... | collective-permute-start | bytes 614408 | tf_op jit(solution)/shard_map/ppermute | solution.py:22
  163.5 32.8 %slice-start = ((s8[6553600]{0:T(1024)(128)(4,1)}), s8[4194304]{0:T(1024)(128)(4,1)S(1)}, s32[]{:S(2)}) async-start(s8[6553600]{0:T(1024)(128)(4,1)} %bitcast.18), calls=%async_computation.4 | async-start | bytes 8388608
  163.6 32.6 %slice-start.1 = ((s8[6553600]{0:T(1024)(128)(4,1)}), s8[2359296]{0:T(1024)(128)(4,1)S(1)}, s32[]{:S(2)}) async-start(s8[6553600]{0:T(1024)(128)(4,1)} %bitcast.18), calls=%async_computation.5 | async-start | bytes 4718592
  168.1 7.5 %collective-permute-start.7 = (bf16[160,640]{1,0:T(8,128)(2,1)S(1)}, bf16[160,640]{1,0:T(8,128)(2,1)S(1)}, u32[]{:S(2)}, u32[]{:S(2)}) collective-permute-start(bf16[160,640]{1,0:T(8,128)(2,1)S(1)} %get-tuple-element.30), channel_id=1, source_target_pairs={{0,1},{1,2},{2,3},{3,4},{4,5},{5,6},{6,7},{7,0},{8,9},{9,10},{10,1... | collective-permute-start | bytes 614408 | tf_op jit(solution)/shard_map/ppermute | solution.py:22
  169.9 7.2 %collective-permute-start.8 = (bf16[160,640]{1,0:T(8,128)(2,1)S(1)}, bf16[160,640]{1,0:T(8,128)(2,1)S(1)}, u32[]{:S(2)}, u32[]{:S(2)}) collective-permute-start(bf16[160,640]{1,0:T(8,128)(2,1)S(1)} %get-tuple-element.30), channel_id=1, source_target_pairs={{0,7},{1,0},{2,1},{3,2},{4,3},{5,4},{6,5},{7,6},{8,15},{9,8},{10,9... | collective-permute-start | bytes 614408 | tf_op jit(solution)/shard_map/ppermute | solution.py:27
  175.6 6.9 %collective-permute-start.9 = (bf16[160,640]{1,0:T(8,128)(2,1)S(1)}, bf16[160,640]{1,0:T(8,128)(2,1)S(1)}, u32[]{:S(2)}, u32[]{:S(2)}) collective-permute-start(bf16[160,640]{1,0:T(8,128)(2,1)S(1)} %collective-permute-done.7), channel_id=1, source_target_pairs={{0,1},{1,2},{2,3},{3,4},{4,5},{5,6},{6,7},{7,0},{8,9},{9,10},{10,1... | collective-permute-start | bytes 614408 | tf_op jit(solution)/shard_map/ppermute | solution.py:22
  177.2 6.9 %collective-permute-start.10 = (bf16[160,640]{1,0:T(8,128)(2,1)S(1)}, bf16[160,640]{1,0:T(8,128)(2,1)S(1)}, u32[]{:S(2)}, u32[]{:S(2)}) collective-permute-start(bf16[160,640]{1,0:T(8,128)(2,1)S(1)} %collective-permute-done.8), channel_id=1, source_target_pairs={{0,7},{1,0},{2,1},{3,2},{4,3},{5,4},{6,5},{7,6},{8,15},{9,8},{10,9... | collective-permute-start | bytes 614408 | tf_op jit(solution)/shard_map/ppermute | solution.py:27
  182.5 7.0 %collective-permute-start.11 = (bf16[160,640]{1,0:T(8,128)(2,1)S(1)}, bf16[160,640]{1,0:T(8,128)(2,1)S(1)}, u32[]{:S(2)}, u32[]{:S(2)}) collective-permute-start(bf16[160,640]{1,0:T(8,128)(2,1)S(1)} %collective-permute-done.9), channel_id=1, source_target_pairs={{0,1},{1,2},{2,3},{3,4},{4,5},{5,6},{6,7},{7,0},{8,9},{9,10},{10,1... | collective-permute-start | bytes 614408 | tf_op jit(solution)/shard_map/ppermute | solution.py:22
  184.1 6.7 %collective-permute-start.12 = (bf16[160,640]{1,0:T(8,128)(2,1)S(1)}, bf16[160,640]{1,0:T(8,128)(2,1)S(1)}, u32[]{:S(2)}, u32[]{:S(2)}) collective-permute-start(bf16[160,640]{1,0:T(8,128)(2,1)S(1)} %collective-permute-done.10), channel_id=1, source_target_pairs={{0,7},{1,0},{2,1},{3,2},{4,3},{5,4},{6,5},{7,6},{8,15},{9,8},{10,9... | collective-permute-start | bytes 614408 | tf_op jit(solution)/shard_map/ppermute | solution.py:27
  189.5 6.7 %collective-permute-start.13 = (bf16[160,640]{1,0:T(8,128)(2,1)S(1)}, bf16[160,640]{1,0:T(8,128)(2,1)S(1)}, u32[]{:S(2)}, u32[]{:S(2)}) collective-permute-start(bf16[160,640]{1,0:T(8,128)(2,1)S(1)} %collective-permute-done.11), channel_id=1, source_target_pairs={{0,1},{1,2},{2,3},{3,4},{4,5},{5,6},{6,7},{7,0},{8,9},{9,10},{10,1... | collective-permute-start | bytes 614408 | tf_op jit(solution)/shard_map/ppermute | solution.py:22
Sparse Core Ops, SparseCore 0:
  11.1 57.0 all-gather.2
  103.1 60.3 all-gather.4
